TPU v7x, 32 devices: a whole 2x2x4 slice. The times are simulated.
32 devices in a mesh: grp: 4 (over z), seq: 8 (over y, x, core).
Axes of the slice: x: 2, y: 2, z: 4, core: 2. Of those that a mesh axis runs over, the one named last changes fastest.
Arguments:
- latent: bfloat16 [4, 256, 32, 256], P('grp', 'seq'), may hold values from -6 to 6
- up_key: bfloat16 [4, 128, 256], replicated, may hold values from -0.5 to 0.5
- up_value: bfloat16 [4, 128, 256], replicated, may hold values from -0.5 to 0.5
- queries: bfloat16 [8, 64, 128], replicated, may hold values from -240 to 240, as said below
- lengths: int32 [8], replicated, may hold values from 1 to 1024
- block_dest: int32 [256], replicated, may hold values from 0 to 31, as said below
Outputs:
- decode_latent: bfloat16 [32, 4, 8, 32, 256], P(('grp', 'seq'))
- attended: float32 [8, 8192], replicated
Inputs may be any that keep to these rules, and one draw needn't show every extreme that they name: `block_dest`: each aligned run of 32 entries (the blocks of one seq index in the prefill layout) names every decode device exactly once. `queries`: the new token's query entries, real-valued.
All inputs are finite; a program needn't handle non-finite values.
Results may differ from a plain program's by a relative error of at most 0.001.
Values may be sent and summed in bfloat16 or wider, within the bound.
A program may use at most 64 MiB of HBM per device.

v0:
```python
import jax
import jax.numpy as jnp
from jax import lax
from jax.sharding import PartitionSpec as P


def joined(x, axis, combine):
    everything = jax.tree.map(lambda part: lax.all_gather(part, axis), x)
    leading = jax.tree.map(lambda part: part[0], everything)

    def lap(k, so_far):
        return combine(so_far, jax.tree.map(lambda part: part[k], everything))

    return lax.fori_loop(1, lax.axis_size(axis), lap, leading)


def combine(first, second):
    largest = jnp.maximum(first[0], second[0])
    factor_a = jnp.exp(first[0] - largest)
    factor_b = jnp.exp(second[0] - largest)
    totals = first[1] * factor_a + second[1] * factor_b
    accum = first[2] * factor_a[..., None] + second[2] * factor_b[..., None]
    return (largest, totals, accum)


def slot_info(global_ids, lengths, block_len, blk_seq, batch):
    seq_ids = global_ids // blk_seq
    starts = global_ids % blk_seq * block_len
    positions = starts[:, None] + jnp.arange(block_len, dtype=jnp.int32)[None, :]
    seq_hot = (seq_ids[:, None] == jnp.arange(batch, dtype=jnp.int32)[None, :]).astype(jnp.int32)
    slot_len = jnp.sum(seq_hot * lengths[None, :], axis=1)
    live = positions < slot_len[:, None]
    return (seq_hot, live)


def partials(cache, key_map, value_map, slot_query, live, seq_hot):
    rank = cache.shape[3] // 2
    head_dim = slot_query.shape[-1]
    scale = 1.0 / float(head_dim) ** 0.5
    highest = lax.Precision.HIGHEST
    key_lat = cache[..., :rank]
    value_lat = cache[..., rank:]
    keys = jnp.einsum("gstr,grkd->gstkd", key_lat, key_map, preferred_element_type=jnp.float32)
    scores = (
        jnp.einsum("gstkd,sgkjd->gskjt", keys, slot_query.astype(jnp.float32), precision=highest)
        * scale
    )
    live_wide = live[None, :, None, None, :]
    scores = jnp.where(live_wide, scores, -1e30)
    slot_max = jnp.max(scores, axis=-1)
    weights = jnp.where(live_wide, jnp.exp(scores - slot_max[..., None]), 0.0)
    slot_tot = jnp.sum(weights, axis=-1)
    values = jnp.einsum(
        "gstr,grkd->gstkd", value_lat, value_map, preferred_element_type=jnp.float32
    )
    slot_acc = jnp.einsum("gskjt,gstkd->gskjd", weights, values, precision=highest)
    hot_bool = seq_hot > 0
    hot_float = seq_hot.astype(jnp.float32)
    spread = jnp.where(hot_bool[None, :, None, None, :], slot_max[..., None], -1e30)
    seq_max = jnp.max(spread, axis=1)
    slot_seq_max = jnp.sum(
        jnp.where(hot_bool[None, :, None, None, :], seq_max[:, None], 0.0), axis=-1
    )
    factor = jnp.exp(slot_max - slot_seq_max)
    totals = jnp.einsum("gskj,sb->gkjb", slot_tot * factor, hot_float, precision=highest)
    accum = jnp.einsum(
        "gskjd,sb->gkjbd", slot_acc * factor[..., None], hot_float, precision=highest
    )
    return (seq_max, totals, accum)


def body(latent, up_key, up_value, queries, lengths, block_dest):
    groups = up_key.shape[0]
    dests = latent.shape[1]
    block_len = latent.shape[2]
    rank = latent.shape[3] // 2
    shards = block_dest.shape[0] // dests
    batch = queries.shape[0]
    q_heads = queries.shape[1]
    head_dim = queries.shape[2]
    per_group = up_key.shape[2] // head_dim
    per_kv = q_heads // (groups * per_group)
    blk_seq = block_dest.shape[0] // batch
    own_shard = lax.axis_index("seq")
    own_dests = lax.dynamic_slice_in_dim(block_dest, own_shard * dests, dests)
    source_order = (
        jnp.zeros((dests,), jnp.int32).at[own_dests].set(jnp.arange(dests, dtype=jnp.int32))
    )
    outgoing = latent[0][source_order]
    received = lax.all_to_all(outgoing, ("grp", "seq"), split_axis=0, concat_axis=0, tiled=True)
    received = received.reshape(groups, shards, block_len, 2 * rank)
    decode_latent = received[None]
    key_map = up_key.reshape(groups, rank, per_group, head_dim)
    value_map = up_value.reshape(groups, rank, per_group, head_dim)
    query_rows = queries.reshape(batch, q_heads * head_dim)
    own_group = lax.axis_index("grp")
    slots = latent.shape[1]
    global_ids = own_shard * slots + jnp.arange(slots, dtype=jnp.int32)
    seq_hot, live = slot_info(global_ids, lengths, block_len, blk_seq, batch)
    picked = jnp.dot(seq_hot.astype(jnp.bfloat16), query_rows, preferred_element_type=jnp.float32)
    slot_query = picked.astype(jnp.bfloat16).reshape(slots, groups, per_group, per_kv, head_dim)
    group_query = lax.dynamic_slice_in_dim(slot_query, own_group, 1, 1)
    group_key = lax.dynamic_slice_in_dim(key_map, own_group, 1, 0)
    group_value = lax.dynamic_slice_in_dim(value_map, own_group, 1, 0)
    local = partials(latent, group_key, group_value, group_query, live, seq_hot)
    merged = joined(local, "seq", combine)
    part_result = merged[2] / merged[1][..., None]
    result = lax.all_gather(part_result, "grp", axis=0, tiled=True)
    attended = jnp.transpose(result, (3, 0, 1, 2, 4)).reshape(batch, q_heads * head_dim)
    return (decode_latent, attended)


def solution(mesh):
    return jax.shard_map(
        body,
        mesh=mesh,
        in_specs=(P("grp", "seq", None, None), P(), P(), P(), P(), P()),
        out_specs=(P(("grp", "seq"), None, None, None, None), P()),
        check_vma=False,
    )
```

profile of v0, /device:TPU:0, one launch (start us, length us, event | category | flops | bytes accessed | tf_op | source)
XLA Modules:
  0.0 64.5 jit_solution(13679540145000248874)
XLA Ops:
  0.6 0.0 copy-start.4
  0.6 0.7 %copy-done.4 = s32[256]{0:T(256)S(1)} copy-done((s32[256]{0:T(256)S(1)}, s32[256]{0:T(256)}, u32[]{:S(2)}) %copy-start.4) | copy-done | bytes 1048
  1.3 0.1 compare_select_fusion.1
  1.4 0.7 %scatter_custom_fusion = s32[32]{0:T(128)S(1)} fusion(s32[32]{0:T(128)S(1)} %compare_select_fusion.1, s32[32]{0:T(128)S(1)} %iota.27, s32[]{:T(128)} %constant.75.clone.1), kind=kCustom, calls=%fused_computation.69 | custom fusion | bytes 132 | tf_op jit(solution)/shard_map/scatter | solution.py:87
  2.1 2.4 %gather_fusion = bf16[32,32,256]{2,1,0:T(8,128)(2,1)} fusion(bf16[32,32,256]{2,1,0:T(8,128)(2,1)} %bitcast.100, s32[1024]{0:T(1024)S(1)} %pad_clamp_fusion), kind=kCustom, calls=%fused_computation | custom fusion | bytes 1048704 | tf_op jit(solution)/shard_map/gather | solution.py:89
  4.5 0.0 copy-start.1
  4.5 7.3 %all-to-all-start = ((bf16[32,32,256]{2,1,0:T(8,128)(2,1)}), bf16[32,32,256]{2,1,0:T(8,128)(2,1)S(1)}, u32[]{:S(2)}, u32[]{:S(2)}) async-start(bf16[32,32,256]{2,1,0:T(8,128)(2,1)} %gather_fusion), calls=%async_computation | async-start | bytes 1048576 | tf_op jit(solution)/shard_map/all_to_all | solution.py:90
  11.9 0.0 copy-start.5
  11.9 0.6 copy-done.5
  12.5 0.1 select_reduce_fusion.2
  12.6 0.0 copy-done.1
  12.6 0.0 copy-start.2
  12.6 0.1 reshape.227
  12.7 0.9 %copy-done.2 = bf16[4,128,256]{2,1,0:T(8,128)(2,1)S(1)} copy-done((bf16[4,128,256]{2,1,0:T(8,128)(2,1)S(1)}, bf16[4,128,256]{2,1,0:T(8,128)(2,1)}, u32[]{:S(2)}) %copy-start.2) | copy-done | bytes 262168
  13.6 0.0 copy-start
  13.6 0.1 reshape.230
  13.6 0.1 constant_dynamic-slice_fusion
  13.7 0.9 %copy-done = bf16[1,32,32,256]{3,2,1,0:T(8,128)(2,1)S(1)} copy-done((bf16[1,32,32,256]{3,2,1,0:T(8,128)(2,1)S(1)}, bf16[1,32,32,256]{3,2,1,0:T(8,128)(2,1)}, u32[]{:S(2)}) %copy-start) | copy-done | bytes 524312
  14.6 0.0 copy-start.3
  14.6 0.3 convolution_bitcast_fusion.1
  14.9 0.6 copy-done.3
  15.5 0.3 fusion.5
  15.9 0.1 copy.47
  16.0 0.1 add_compare_fusion
  16.1 1.1 %fusion.35 = (f32[32,2,8]{2,1,0:T(2,128)S(1)}, f32[32,2,8,32]{3,2,1,0:T(8,128)S(1)}) fusion(f32[32,32,2,128]{3,1,2,0:T(8,128)S(1)} %convolution_bitcast_fusion.1, bf16[32,4,2,8,128]{4,3,2,1,0:T(8,128)(2,1)S(1)} %bitcast.103, s32[]{:T(128)S(6)} %select_n.84, pred[32,32]{1,0:T(8,128)(4,1)S(1)} %add_compare_fusion), kind=kOutput, calls=%fused_computation.72 | convolution fusion | flops 25214464 | bytes 1251332 | tf_op jit(solution)/shard_map/gstkd,sgkjd->gskjt/dot_general | solution.py:45
  17.1 0.1 copy.31
  17.2 0.1 select_reduce_fusion.1
  17.3 0.1 select_reduce_fusion
  17.4 9.8 %all-gather = f32[16,8,8]{2,1,0:T(8,128)S(1)} all-gather(f32[2,8,8]{2,1,0:T(8,128)S(1)} %select_reduce_fusion.1), channel_id=2, replica_groups=mesh['grp'=4,'seq'=8] {'seq'}, dimensions={0}, use_global_device_ids=true | all-gather | bytes 4608 | tf_op jit(solution)/shard_map/all_gather | solution.py:8
  27.2 0.1 copy.36
  27.3 0.3 convolution_bitcast_fusion
  27.6 0.3 fusion.13
  27.8 1.1 %convolution_multiply_fusion = f32[32,2,8,128]{3,2,1,0:T(8,128)S(1)} fusion(f32[32,32,2,128]{3,1,0,2:T(8,128)S(1)} %convolution_bitcast_fusion, f32[32,2,8,32]{3,2,1,0:T(8,128)S(1)} %get-tuple-element.228, f32[32,2,8]{2,1,0:T(2,128)S(1)} %copy.36, f32[32,2,8]{2,1,0:T(2,128)S(1)} %get-tuple-element.227, pred[32,32]{1,0:T(8,128)(4,1)S(1)} %add_compare_fusion), kind=kOutput, calls=%fused_computation.16 | convolution fusion | flops 25264128 | bytes 1381376 | tf_op jit(solution)/shard_map/gskjt,gstkd->gskjd/dot_general | solution.py:56
  28.9 0.3 convolution_bitcast_fusion.2
  29.2 9.7 %all-gather.2 = f32[8,2,8,8,128]{4,3,2,1,0:T(8,128)S(1)} all-gather(f32[1,2,8,8,128]{4,3,2,1,0:T(8,128)S(1)} %convolution_bitcast_fusion.2), channel_id=4, replica_groups=mesh['grp'=4,'seq'=8] {'seq'}, dimensions={0}, use_global_device_ids=true | all-gather | bytes 589824 | tf_op jit(solution)/shard_map/all_gather | solution.py:8
  38.9 0.1 copy.33
  39.0 0.1 fusion.21
  39.1 8.4 %all-gather.1 = f32[16,8,8]{2,1,0:T(8,128)S(1)} all-gather(f32[2,8,8]{2,1,0:T(8,128)S(1)} %fusion.21), channel_id=3, replica_groups=mesh['grp'=4,'seq'=8] {'seq'}, dimensions={0}, use_global_device_ids=true | all-gather | bytes 4608 | tf_op jit(solution)/shard_map/all_gather | solution.py:8
  47.5 1.4 %while.19 = (s32[]{:T(128)}, f32[1,2,8,8]{3,2,1,0:T(8,128)S(1)}, f32[1,2,8,8]{3,2,1,0:T(8,128)S(1)}, f32[1,2,8,8,128]{4,3,2,1,0:T(8,128)S(1)}, f32[8,1,2,8,8]{4,...) while((s32[]{:T(128)}, f32[1,2,8,8]{3,2,1,0:T(8,128)S(1)}, ...), condition=%wide.region_7.8_spmd, body=%wide.region_6.7_spmd.sunk | while | flops 50053 | bytes 204443 | solution.py:14
  47.6 0.1 fusion.42
  47.7 0.1 fusion.42
  47.9 0.1 fusion.42
  48.1 0.1 fusion.42
  48.3 0.1 fusion.42
  48.5 0.1 fusion.42
  48.7 0.1 fusion.42
  48.9 0.1 broadcast_divide_fusion
  49.0 14.0 %all_gather.27 = f32[4,2,8,8,128]{4,3,2,1,0:T(8,128)S(1)} all-gather(f32[1,2,8,8,128]{4,3,2,1,0:T(8,128)S(1)} %broadcast_divide_fusion), channel_id=1, replica_groups=mesh['grp'=4,'seq'=8] {'grp'}, dimensions={0}, use_global_device_ids=true | all-gather | bytes 327680 | tf_op jit(solution)/shard_map/all_gather | solution.py:108
  63.0 0.0 all-to-all-done
  63.0 0.8 %copy.74 = bf16[1,4,8,32,256]{4,3,2,1,0:T(8,128)(2,1)} copy(bf16[1,4,8,32,256]{4,3,2,1,0:T(8,128)(2,1)S(1)} %bitcast.99) | data formatting | bytes 1048576
  63.8 0.7 %copy.75 = f32[8,8192]{1,0:T(8,128)} copy(f32[8,8192]{1,0:T(8,128)S(1)} %bitcast.102) | data formatting | bytes 524288
  (30 shorter events, 0.3 us)
Async XLA Ops:
  0.6 0.7 %copy-start.4 = (s32[256]{0:T(256)S(1)}, s32[256]{0:T(256)}, u32[]{:S(2)}) copy-start(s32[256]{0:T(256)} %param.13) | copy-start | bytes 3076
  4.5 8.1 %copy-start.1 = (bf16[4,128,256]{2,1,0:T(8,128)(2,1)S(1)}, bf16[4,128,256]{2,1,0:T(8,128)(2,1)}, u32[]{:S(2)}) copy-start(bf16[4,128,256]{2,1,0:T(8,128)(2,1)} %param.9) | copy-start | bytes 786436
  4.5 58.4 %all-to-all-start = ((bf16[32,32,256]{2,1,0:T(8,128)(2,1)}), bf16[32,32,256]{2,1,0:T(8,128)(2,1)S(1)}, u32[]{:S(2)}, u32[]{:S(2)}) async-start(bf16[32,32,256]{2,1,0:T(8,128)(2,1)} %gather_fusion), calls=%async_computation | async-start | bytes 1048576 | tf_op jit(solution)/shard_map/all_to_all | solution.py:90
  11.9 0.7 %copy-start.5 = (s32[8]{0:T(128)S(1)}, s32[8]{0:T(128)}, u32[]{:S(2)}) copy-start(s32[8]{0:T(128)} %param.12) | copy-start | bytes 100
  12.6 1.0 %copy-start.2 = (bf16[4,128,256]{2,1,0:T(8,128)(2,1)S(1)}, bf16[4,128,256]{2,1,0:T(8,128)(2,1)}, u32[]{:S(2)}) copy-start(bf16[4,128,256]{2,1,0:T(8,128)(2,1)} %param.10) | copy-start | bytes 786436
  13.6 1.0 %copy-start = (bf16[1,32,32,256]{3,2,1,0:T(8,128)(2,1)S(1)}, bf16[1,32,32,256]{3,2,1,0:T(8,128)(2,1)}, u32[]{:S(2)}) copy-start(bf16[1,32,32,256]{3,2,1,0:T(8,128)(2,1)} %param.8) | copy-start | bytes 1572868
  14.6 0.9 %copy-start.3 = (bf16[8,64,128]{2,1,0:T(8,128)(2,1)S(1)}, bf16[8,64,128]{2,1,0:T(8,128)(2,1)}, u32[]{:S(2)}) copy-start(bf16[8,64,128]{2,1,0:T(8,128)(2,1)} %param.11) | copy-start | bytes 393220
where the time goes:
time: 64.9 us; the launch traced here: 64.5 us
  blocking collectives  41.9 us (65%)
  local copies, waits for them, and re-layouts  8.87 us (14%)
  starting transfers between devices  7.33 us (11%)
  matrix products  3.45 us (5%)
  other arithmetic  1.85 us (3%)
  between operations  0.79 us (1%)
    all_gather x3, blocking collectives, joined(): everything = jax.tree.map(lambda part: lax.all_gather(part, axis), x)  27.9 us
    all_gather x1, blocking collectives, body(): result = lax.all_gather(part_result, 'grp', axis=0, tiled=True)  14 us
    all_to_all x1, starting transfers between devices, body(): lax.all_to_all(outgoing, ('grp', 'seq'), split_axis=0, concat_axis=0, til...  7.33 us
    unnamed x15, local copies, waits for them, and re-layouts  5.29 us
    gather x1, local copies, waits for them, and re-layouts, body(): outgoing = latent[0][source_order]  2.42 us
  transfers between devices with their start and end apart: 1, of which 0 were waited for; matrix products, arithmetic and copies ran while one was open for 9% of the time, Pallas kernels for 0%

commit v1 on v0

v1 whole, which is shorter than its diff:
```python
import functools

import jax
import jax.numpy as jnp
from jax import lax
from jax.experimental import pallas as pl
from jax.experimental.pallas import tpu as pltpu
from jax.sharding import PartitionSpec as P

MESH = pl.DeviceIdType.MESH


def pieces(x):
    high = x.astype(jnp.bfloat16)
    rest = x - high.astype(jnp.float32)
    middle = rest.astype(jnp.bfloat16)
    low = (rest - middle.astype(jnp.float32)).astype(jnp.bfloat16)
    return jnp.concatenate([high, middle, low], axis=0)


def dot_pieces(x, y, dims):
    rows = x.shape[0]
    out = lax.dot_general(pieces(x), y, (dims, ((), ())), preferred_element_type=jnp.float32)
    return out[:rows] + (out[rows : 2 * rows] + out[2 * rows :])


def local_kernel(per_seq, per_group, per_kv, dest_ref, len_ref, lat_ref, q_ref, uk_ref, uv_ref, out_ref, part_ref):
    own_group = lax.axis_index("grp")
    own_shard = lax.axis_index("seq")
    slots, block_len, width = lat_ref.shape[1:]
    rank = width // 2
    head_dim = q_ref.shape[2]
    heads = per_group * per_kv

    @pl.loop(0, slots)
    def _(i):
        out_ref[dest_ref[own_shard * slots + i]] = lat_ref[0, i]

    sequence = own_shard // per_seq
    offset = (own_shard - sequence * per_seq) * (slots * block_len)
    left = len_ref[sequence] - offset
    tokens = slots * block_len
    query = q_ref[sequence, pl.ds(pl.multiple_of(own_group * heads, heads), heads), :]
    key_map = uk_ref[own_group]
    value_map = uv_ref[own_group]

    def cols(m, k):
        return m[:, k * head_dim : (k + 1) * head_dim]

    def rows(m, k):
        return m[k * per_kv : (k + 1) * per_kv]

    absorbed = jnp.concatenate(
        [
            rows(
                lax.dot_general(query, cols(key_map, k), (((1,), (1,)), ((), ())), preferred_element_type=jnp.float32),
                k,
            )
            for k in range(per_group)
        ],
        axis=0,
    )
    key_lat = lat_ref[0, :, :, :rank].reshape(tokens, rank)
    value_lat = lat_ref[0, :, :, rank:].reshape(tokens, rank)
    scores = dot_pieces(absorbed, key_lat, ((1,), (1,))) * (1.0 / float(head_dim) ** 0.5)
    live = lax.broadcasted_iota(jnp.int32, (heads, tokens), 1) < left
    scores = jnp.where(live, scores, -1e30)
    largest = jnp.max(scores, axis=1, keepdims=True)
    weights = jnp.where(live, jnp.exp(scores - largest), 0.0)
    total = jnp.sum(weights, axis=1, keepdims=True)
    some = jnp.where(total > 0.0, total, 1.0)
    mixed = dot_pieces(weights, value_lat, ((1,), (0,))) / some
    part_ref[0:heads, :] = jnp.concatenate(
        [rows(dot_pieces(mixed, cols(value_map, k), ((1,), (0,))), k) for k in range(per_group)], axis=0
    )
    if per_seq > 1:
        size = jnp.where(total > 0.0, largest + jnp.log(some), -1e30)
        part_ref[heads : 2 * heads, :] = jnp.broadcast_to(size, (heads, head_dim))


def comm_kernel(grps, seqs, out_ref, part_ref, recv_ref, all_ref, send_a, recv_a, send_b, recv_b):
    n = grps * seqs
    me = lax.axis_index("grp") * seqs + lax.axis_index("seq")
    barrier = pltpu.get_barrier_semaphore()

    def place(k):
        to = lax.rem(me + k, n)
        return to, (to // seqs, lax.rem(to, seqs))

    @pl.loop(1, n)
    def _(k):
        pl.semaphore_signal(barrier, inc=1, device_id=place(k)[1], device_id_type=MESH)

    pl.semaphore_wait(barrier, n - 1)

    @pl.loop(1, n)
    def _(k):
        to, there = place(k)
        pltpu.make_async_remote_copy(
            src_ref=part_ref, dst_ref=all_ref.at[me], send_sem=send_b, recv_sem=recv_b,
            device_id=there, device_id_type=MESH,
        ).start()
        pltpu.make_async_remote_copy(
            src_ref=out_ref.at[to], dst_ref=recv_ref.at[me], send_sem=send_a, recv_sem=recv_a,
            device_id=there, device_id_type=MESH,
        ).start()

    recv_ref[me] = out_ref[me]
    all_ref[me] = part_ref[...]
    most = pl.ds(0, n - 1)
    for ref, sems in ((all_ref, (send_b, recv_b)), (recv_ref, (send_a, recv_a))):
        for sem in sems:
            pltpu.make_async_copy(ref.at[most], ref.at[most], sem).wait()


def body(grps, seqs, latent, up_key, up_value, queries, lengths, block_dest):
    groups = up_key.shape[0]
    slots, block_len, width = latent.shape[1:]
    batch, q_heads, head_dim = queries.shape
    per_group = up_key.shape[2] // head_dim
    heads = q_heads // groups
    per_kv = heads // per_group
    n = grps * seqs
    blk_seq = block_dest.shape[0] // batch
    per_seq = blk_seq // slots
    assert per_seq * slots == blk_seq and n == slots and groups == grps
    part_rows = heads if per_seq == 1 else 2 * heads
    vmem = pl.BlockSpec(memory_space=pltpu.VMEM)
    smem = pl.BlockSpec(memory_space=pltpu.SMEM)
    outgoing, part = pl.pallas_call(
        functools.partial(local_kernel, per_seq, per_group, per_kv),
        out_shape=(
            jax.ShapeDtypeStruct((slots, block_len, width), latent.dtype),
            jax.ShapeDtypeStruct((part_rows, head_dim), jnp.float32),
        ),
        in_specs=[smem, smem, vmem, vmem, vmem, vmem],
        out_specs=(vmem, vmem),
        name="local_part",
    )(block_dest, lengths, latent, queries, up_key, up_value)
    received, everything = pl.pallas_call(
        functools.partial(comm_kernel, grps, seqs),
        out_shape=(
            jax.ShapeDtypeStruct((n, block_len, width), latent.dtype),
            jax.ShapeDtypeStruct((n, part_rows, head_dim), jnp.float32),
        ),
        in_specs=[vmem, vmem],
        out_specs=(vmem, vmem),
        scratch_shapes=[pltpu.SemaphoreType.DMA] * 4,
        compiler_params=pltpu.CompilerParams(collective_id=0, has_side_effects=True),
        name="exchange",
    )(outgoing, part)
    decode_latent = received.reshape(1, groups, seqs, block_len, width)
    parts = everything.reshape(groups, batch, per_seq, part_rows, head_dim)
    result = parts[:, :, 0, :heads]
    if per_seq > 1:
        sizes = parts[:, :, :, heads:]
        share = jax.nn.softmax(sizes, axis=2)
        result = jnp.sum(parts[:, :, :, :heads] * share, axis=2)
    attended = jnp.transpose(result, (1, 0, 2, 3)).reshape(batch, q_heads * head_dim)
    return (decode_latent, attended)


def solution(mesh):
    return jax.shard_map(
        functools.partial(body, mesh.shape["grp"], mesh.shape["seq"]),
        mesh=mesh,
        in_specs=(P("grp", "seq", None, None), P(), P(), P(), P(), P()),
        out_specs=(P(("grp", "seq"), None, None, None, None), P()),
        check_vma=False,
    )
```

time: 64.9 us -> 31.3 us (0.48)
  the two profiles are of different devices: /device:TPU:0 before, /device:TPU:15 now
where the time goes in v1:
time: 31.3 us; the launch traced here: 31.1 us
  Pallas kernels  27.9 us (89%)
  local copies, waits for them, and re-layouts  2.59 us (8%)
  between operations  0.65 us (2%)
    pallas_call x1, Pallas kernels, body(): pl.pallas_call(functools.partial(comm_kernel, grps, seqs), out_shape=(jax...  25.1 us
    pallas_call x1, Pallas kernels, body(): pl.pallas_call(functools.partial(local_kernel, per_seq, per_group, per_kv...  2.79 us
    transpose x1, local copies, waits for them, and re-layouts, body(): jnp.transpose(result, (1, 0, 2, 3)).reshape(batch, q_heads * head_dim)  1.79 us
    unnamed x3, local copies, waits for them, and re-layouts  0.8 us

profile of v1, /device:TPU:15, one launch (start us, length us, event | category | flops | bytes accessed | tf_op | source)
XLA Modules:
  0.0 31.1 jit_solution(11316856825770408307)
XLA Ops:
  0.6 2.8 %local_part.1 = (bf16[32,32,256]{2,1,0:T(8,128)(2,1)}, f32[16,128]{1,0:T(8,128)}) custom-call(s32[256]{0:T(256)} %dest_ref.1, s32[8]{0:T(128)} %len_ref.1, bf16[1,32,32,256]{3,2,1,0:T(8,128)(2,1)} %lat_ref.1, bf16[8,64,128]{2,1,0:T(8,128)(2,1)} %q_ref.1, bf16[4,128,256]{2,1,0:T(8,128)(2,1)} %uk_ref.1, bf16[4,128,256]{2,1,0:T(8,128)(2,1)} %uv_ref.1), custom_call_target="tpu_custom_call" | custom-call | tf_op jit(solution)/shard_map/local_part/pallas_call | solution.py:130
  3.4 25.1 %exchange.1 = (bf16[32,32,256]{2,1,0:T(8,128)(2,1)}, f32[32,16,128]{2,1,0:T(8,128)}) custom-call(bf16[32,32,256]{2,1,0:T(8,128)(2,1)} %get-tuple-element.6.out_ref, f32[16,128]{1,0:T(8,128)} %get-tuple-element.7.part_ref), custom_call_target="tpu_custom_call" | custom-call | tf_op jit(solution)/shard_map/exchange/pallas_call | solution.py:140
  28.5 0.0 copy-start
  28.5 1.8 %copy.8 = f32[8,4,16,128]{3,0,2,1:T(8,128)} copy(f32[8,4,16,128]{3,2,0,1:T(8,128)} %bitcast.7) | data formatting | bytes 524288 | tf_op jit(solution)/shard_map/transpose | solution.py:159
  30.3 0.0 copy-done
  30.3 0.8 %copy.10 = bf16[1,4,8,32,256]{4,3,2,1,0:T(8,128)(2,1)} copy(bf16[1,4,8,32,256]{4,3,2,1,0:T(8,128)(2,1)S(1)} %bitcast.5) | data formatting | bytes 1048576
Async XLA Ops:
  28.5 1.8 %copy-start = (bf16[32,32,256]{2,1,0:T(8,128)(2,1)S(1)}, bf16[32,32,256]{2,1,0:T(8,128)(2,1)}, u32[]{:S(2)}) copy-start(bf16[32,32,256]{2,1,0:T(8,128)(2,1)} %get-tuple-element.8) | copy-start | bytes 1572868

commit v2 on v1

--- a/solution.py
+++ b/solution.py
@@ -78,14 +78,22 @@
         part_ref[heads : 2 * heads, :] = jnp.broadcast_to(size, (heads, head_dim))
 
 
-def comm_kernel(grps, seqs, out_ref, part_ref, recv_ref, all_ref, send_a, recv_a, send_b, recv_b):
+def comm_kernel(grps, seqs, out_ref, part_ref, recv_ref, all_ref, send_a, recv_a, send_b, recv_b, recv_z):
     n = grps * seqs
-    me = lax.axis_index("grp") * seqs + lax.axis_index("seq")
+    group = lax.axis_index("grp")
+    shard = lax.axis_index("seq")
+    me = group * seqs + shard
+    mine = shard * grps + group
     barrier = pltpu.get_barrier_semaphore()
 
     def place(k):
         to = lax.rem(me + k, n)
         return to, (to // seqs, lax.rem(to, seqs))
+
+    def send(src, dst, there, send_sem, recv_sem):
+        pltpu.make_async_remote_copy(
+            src_ref=src, dst_ref=dst, send_sem=send_sem, recv_sem=recv_sem, device_id=there, device_id_type=MESH
+        ).start()
 
     @pl.loop(1, n)
     def _(k):
@@ -93,24 +101,40 @@
 
     pl.semaphore_wait(barrier, n - 1)
 
-    @pl.loop(1, n)
+    @pl.loop(1, grps)
     def _(k):
-        to, there = place(k)
-        pltpu.make_async_remote_copy(
-            src_ref=part_ref, dst_ref=all_ref.at[me], send_sem=send_b, recv_sem=recv_b,
-            device_id=there, device_id_type=MESH,
-        ).start()
-        pltpu.make_async_remote_copy(
-            src_ref=out_ref.at[to], dst_ref=recv_ref.at[me], send_sem=send_a, recv_sem=recv_a,
-            device_id=there, device_id_type=MESH,
-        ).start()
+        send(part_ref, all_ref.at[mine], (lax.rem(group + k, grps), shard), send_b, recv_z)
+
+    @pl.loop(0, n - 1)
+    def _(j):
+        to, there = place(1 + lax.rem(j + n // 2 - 1, n - 1))
+        send(out_ref.at[to], recv_ref.at[me], there, send_a, recv_a)
+
+    @pl.loop(1, seqs)
+    def _(k):
+        send(part_ref, all_ref.at[mine], (group, lax.rem(shard + k, seqs)), send_b, recv_b)
 
     recv_ref[me] = out_ref[me]
-    all_ref[me] = part_ref[...]
-    most = pl.ds(0, n - 1)
-    for ref, sems in ((all_ref, (send_b, recv_b)), (recv_ref, (send_a, recv_a))):
-        for sem in sems:
-            pltpu.make_async_copy(ref.at[most], ref.at[most], sem).wait()
+    all_ref[mine] = part_ref[...]
+
+    def wait(ref, count, sem):
+        some = ref.at[pl.ds(0, count)]
+        pltpu.make_async_copy(some, some, sem).wait()
+
+    wait(all_ref, grps - 1, recv_z)
+
+    @pl.loop(1, grps)
+    def _(j):
+        held = all_ref.at[shard * grps + lax.rem(group + j, grps)]
+
+        @pl.loop(1, seqs)
+        def _(k):
+            send(held, held, (group, lax.rem(shard + k, seqs)), send_b, recv_b)
+
+    wait(all_ref, n - grps, recv_b)
+    wait(recv_ref, n - 1, recv_a)
+    wait(all_ref, n - 1, send_b)
+    wait(recv_ref, n - 1, send_a)
 
 
 def body(grps, seqs, latent, up_key, up_value, queries, lengths, block_dest):
@@ -145,18 +169,17 @@
         ),
         in_specs=[vmem, vmem],
         out_specs=(vmem, vmem),
-        scratch_shapes=[pltpu.SemaphoreType.DMA] * 4,
+        scratch_shapes=[pltpu.SemaphoreType.DMA] * 5,
         compiler_params=pltpu.CompilerParams(collective_id=0, has_side_effects=True),
         name="exchange",
     )(outgoing, part)
     decode_latent = received.reshape(1, groups, seqs, block_len, width)
-    parts = everything.reshape(groups, batch, per_seq, part_rows, head_dim)
-    result = parts[:, :, 0, :heads]
+    parts = everything.reshape(batch, per_seq, groups, part_rows, head_dim)
+    result = parts[:, 0, :, :heads]
     if per_seq > 1:
-        sizes = parts[:, :, :, heads:]
-        share = jax.nn.softmax(sizes, axis=2)
-        result = jnp.sum(parts[:, :, :, :heads] * share, axis=2)
-    attended = jnp.transpose(result, (1, 0, 2, 3)).reshape(batch, q_heads * head_dim)
+        share = jax.nn.softmax(parts[:, :, :, heads:], axis=1)
+        result = jnp.sum(parts[:, :, :, :heads] * share, axis=1)
+    attended = result.reshape(batch, q_heads * head_dim)
     return (decode_latent, attended)
 
 

time: 31.3 us -> 28.5 us (0.911)
  the two profiles are of different devices: /device:TPU:15 before, /device:TPU:0 now
where the time goes in v2:
time: 28.5 us; the launch traced here: 28.3 us
  Pallas kernels  25.1 us (88%)
  local copies, waits for them, and re-layouts  2.56 us (9%)
  between operations  0.65 us (2%)
    pallas_call x1, Pallas kernels, body(): pl.pallas_call(functools.partial(comm_kernel, grps, seqs), out_shape=(jax...  22.3 us
    pallas_call x1, Pallas kernels, body(): pl.pallas_call(functools.partial(local_kernel, per_seq, per_group, per_kv...  2.79 us
    another operation x1, local copies, waits for them, and re-layouts, body(): attended = result.reshape(batch, q_heads * head_dim)  1.76 us
    unnamed x3, local copies, waits for them, and re-layouts  0.8 us

profile of v2, /device:TPU:0, one launch (start us, length us, event | category | flops | bytes accessed | tf_op | source)
XLA Modules:
  0.0 28.3 jit_solution(5778806445757872987)
XLA Ops:
  0.6 2.8 %local_part.1 = (bf16[32,32,256]{2,1,0:T(8,128)(2,1)}, f32[16,128]{1,0:T(8,128)}) custom-call(s32[256]{0:T(256)} %dest_ref.1, s32[8]{0:T(128)} %len_ref.1, bf16[1,32,32,256]{3,2,1,0:T(8,128)(2,1)} %lat_ref.1, bf16[8,64,128]{2,1,0:T(8,128)(2,1)} %q_ref.1, bf16[4,128,256]{2,1,0:T(8,128)(2,1)} %uk_ref.1, bf16[4,128,256]{2,1,0:T(8,128)(2,1)} %uv_ref.1), custom_call_target="tpu_custom_call" | custom-call | tf_op jit(solution)/shard_map/local_part/pallas_call | solution.py:154
  3.4 22.3 %exchange.1 = (bf16[32,32,256]{2,1,0:T(8,128)(2,1)}, f32[32,16,128]{2,1,0:T(8,128)}) custom-call(bf16[32,32,256]{2,1,0:T(8,128)(2,1)} %get-tuple-element.6.out_ref, f32[16,128]{1,0:T(8,128)} %get-tuple-element.7.part_ref), custom_call_target="tpu_custom_call" | custom-call | tf_op jit(solution)/shard_map/exchange/pallas_call | solution.py:164
  25.8 0.0 copy-start
  25.8 1.8 %reshape_squeeze_reshape.3 = f32[8,8192]{1,0:T(8,128)} reshape(f32[32,16,128]{2,1,0:T(8,128)} %get-tuple-element.9) | data formatting | bytes 524288 | tf_op jit(solution)/shard_map/reshape;squeeze;reshape | solution.py:182
  27.5 0.0 copy-done
  27.5 0.8 %copy.9 = bf16[1,4,8,32,256]{4,3,2,1,0:T(8,128)(2,1)} copy(bf16[1,4,8,32,256]{4,3,2,1,0:T(8,128)(2,1)S(1)} %bitcast.1) | data formatting | bytes 1048576
Async XLA Ops:
  25.8 1.8 %copy-start = (bf16[32,32,256]{2,1,0:T(8,128)(2,1)S(1)}, bf16[32,32,256]{2,1,0:T(8,128)(2,1)}, u32[]{:S(2)}) copy-start(bf16[32,32,256]{2,1,0:T(8,128)(2,1)} %get-tuple-element.8) | copy-start | bytes 1572868

commit v3 on v2

--- a/solution.py
+++ b/solution.py
@@ -105,14 +105,21 @@
     def _(k):
         send(part_ref, all_ref.at[mine], (lax.rem(group + k, grps), shard), send_b, recv_z)
 
-    @pl.loop(0, n - 1)
-    def _(j):
-        to, there = place(1 + lax.rem(j + n // 2 - 1, n - 1))
-        send(out_ref.at[to], recv_ref.at[me], there, send_a, recv_a)
+    def block(to_group, to_shard):
+        send(out_ref.at[to_group * seqs + to_shard], recv_ref.at[me], (to_group, to_shard), send_a, recv_a)
+
+    for j in range(grps - 1):
+        step = 1 + (j + grps // 2 - 1) % (grps - 1)
+
+        @pl.loop(0, seqs)
+        def _(k):
+            block(lax.rem(group + step, grps), lax.rem(shard + k, seqs))
 
     @pl.loop(1, seqs)
     def _(k):
-        send(part_ref, all_ref.at[mine], (group, lax.rem(shard + k, seqs)), send_b, recv_b)
+        to_shard = lax.rem(shard + k, seqs)
+        send(part_ref, all_ref.at[mine], (group, to_shard), send_b, recv_b)
+        block(group, to_shard)
 
     recv_ref[me] = out_ref[me]
     all_ref[mine] = part_ref[...]

time: 28.5 us -> 26.3 us (0.923)
  the two profiles are of different devices: /device:TPU:0 before, /device:TPU:15 now
where the time goes in v3:
time: 26.3 us; the launch traced here: 26 us
  Pallas kernels  22.8 us (87%)
  local copies, waits for them, and re-layouts  2.56 us (10%)
  between operations  0.65 us (2%)
    pallas_call x1, Pallas kernels, body(): pl.pallas_call(functools.partial(comm_kernel, grps, seqs), out_shape=(jax...  20 us
    pallas_call x1, Pallas kernels, body(): pl.pallas_call(functools.partial(local_kernel, per_seq, per_group, per_kv...  2.79 us
    another operation x1, local copies, waits for them, and re-layouts, body(): attended = result.reshape(batch, q_heads * head_dim)  1.76 us
    unnamed x3, local copies, waits for them, and re-layouts  0.8 us

profile of v3, /device:TPU:15, one launch (start us, length us, event | category | flops | bytes accessed | tf_op | source)
XLA Modules:
  0.0 26.0 jit_solution(2077802195414509864)
XLA Ops:
  0.6 2.8 %local_part.1 = (bf16[32,32,256]{2,1,0:T(8,128)(2,1)}, f32[16,128]{1,0:T(8,128)}) custom-call(s32[256]{0:T(256)} %dest_ref.1, s32[8]{0:T(128)} %len_ref.1, bf16[1,32,32,256]{3,2,1,0:T(8,128)(2,1)} %lat_ref.1, bf16[8,64,128]{2,1,0:T(8,128)(2,1)} %q_ref.1, bf16[4,128,256]{2,1,0:T(8,128)(2,1)} %uk_ref.1, bf16[4,128,256]{2,1,0:T(8,128)(2,1)} %uv_ref.1), custom_call_target="tpu_custom_call" | custom-call | tf_op jit(solution)/shard_map/local_part/pallas_call | solution.py:161
  3.4 20.0 %exchange.1 = (bf16[32,32,256]{2,1,0:T(8,128)(2,1)}, f32[32,16,128]{2,1,0:T(8,128)}) custom-call(bf16[32,32,256]{2,1,0:T(8,128)(2,1)} %get-tuple-element.6.out_ref, f32[16,128]{1,0:T(8,128)} %get-tuple-element.7.part_ref), custom_call_target="tpu_custom_call" | custom-call | tf_op jit(solution)/shard_map/exchange/pallas_call | solution.py:171
  23.4 0.0 copy-start
  23.4 1.8 %reshape_squeeze_reshape.3 = f32[8,8192]{1,0:T(8,128)} reshape(f32[32,16,128]{2,1,0:T(8,128)} %get-tuple-element.9) | data formatting | bytes 524288 | tf_op jit(solution)/shard_map/reshape;squeeze;reshape | solution.py:189
  25.2 0.0 copy-done
  25.2 0.8 %copy.9 = bf16[1,4,8,32,256]{4,3,2,1,0:T(8,128)(2,1)} copy(bf16[1,4,8,32,256]{4,3,2,1,0:T(8,128)(2,1)S(1)} %bitcast.1) | data formatting | bytes 1048576
Async XLA Ops:
  23.4 1.8 %copy-start = (bf16[32,32,256]{2,1,0:T(8,128)(2,1)S(1)}, bf16[32,32,256]{2,1,0:T(8,128)(2,1)}, u32[]{:S(2)}) copy-start(bf16[32,32,256]{2,1,0:T(8,128)(2,1)} %get-tuple-element.8) | copy-start | bytes 1572868

commit v4 on v3

--- a/solution.py
+++ b/solution.py
@@ -78,7 +78,7 @@
         part_ref[heads : 2 * heads, :] = jnp.broadcast_to(size, (heads, head_dim))
 
 
-def comm_kernel(grps, seqs, out_ref, part_ref, recv_ref, all_ref, send_a, recv_a, send_b, recv_b, recv_z):
+def comm_kernel(grps, seqs, per_seq, out_ref, part_ref, recv_ref, final_ref, all_ref, send_a, recv_a, send_b, recv_b, recv_z):
     n = grps * seqs
     group = lax.axis_index("grp")
     shard = lax.axis_index("seq")
@@ -139,6 +139,15 @@
             send(held, held, (group, lax.rem(shard + k, seqs)), send_b, recv_b)
 
     wait(all_ref, n - grps, recv_b)
+    if per_seq == 1:
+        heads, head_dim = part_ref.shape
+        for g in range(grps):
+            for h in range(heads):
+                start = (g * heads + h) * head_dim
+                taken = [all_ref[b * grps + g, h : h + 1, :] for b in range(seqs)]
+                final_ref[:, start : start + head_dim] = jnp.concatenate(taken, axis=0)
+    else:
+        final_ref[...] = all_ref[...]
     wait(recv_ref, n - 1, recv_a)
     wait(all_ref, n - 1, send_b)
     wait(recv_ref, n - 1, send_a)
@@ -156,6 +165,7 @@
     per_seq = blk_seq // slots
     assert per_seq * slots == blk_seq and n == slots and groups == grps
     part_rows = heads if per_seq == 1 else 2 * heads
+    final_shape = (batch, q_heads * head_dim) if per_seq == 1 else (n, part_rows, head_dim)
     vmem = pl.BlockSpec(memory_space=pltpu.VMEM)
     smem = pl.BlockSpec(memory_space=pltpu.SMEM)
     outgoing, part = pl.pallas_call(
@@ -169,24 +179,23 @@
         name="local_part",
     )(block_dest, lengths, latent, queries, up_key, up_value)
     received, everything = pl.pallas_call(
-        functools.partial(comm_kernel, grps, seqs),
+        functools.partial(comm_kernel, grps, seqs, per_seq),
         out_shape=(
             jax.ShapeDtypeStruct((n, block_len, width), latent.dtype),
-            jax.ShapeDtypeStruct((n, part_rows, head_dim), jnp.float32),
+            jax.ShapeDtypeStruct(final_shape, jnp.float32),
         ),
         in_specs=[vmem, vmem],
         out_specs=(vmem, vmem),
-        scratch_shapes=[pltpu.SemaphoreType.DMA] * 5,
+        scratch_shapes=[pltpu.VMEM((n, part_rows, head_dim), jnp.float32)] + [pltpu.SemaphoreType.DMA] * 5,
         compiler_params=pltpu.CompilerParams(collective_id=0, has_side_effects=True),
         name="exchange",
     )(outgoing, part)
     decode_latent = received.reshape(1, groups, seqs, block_len, width)
-    parts = everything.reshape(batch, per_seq, groups, part_rows, head_dim)
-    result = parts[:, 0, :, :heads]
+    attended = everything
     if per_seq > 1:
+        parts = everything.reshape(batch, per_seq, groups, part_rows, head_dim)
         share = jax.nn.softmax(parts[:, :, :, heads:], axis=1)
-        result = jnp.sum(parts[:, :, :, :heads] * share, axis=1)
-    attended = result.reshape(batch, q_heads * head_dim)
+        attended = jnp.sum(parts[:, :, :, :heads] * share, axis=1).reshape(batch, q_heads * head_dim)
     return (decode_latent, attended)
 
 

time: 26.3 us -> 26.4 us (level)
    unnamed x3 -> x4, local copies, waits for them, and re-layouts: 0.8 us -> 2.62 us
    another operation x1 -> x0, local copies, waits for them, and re-layouts: 1.76 us -> none  [body(): attended = result.reshape(batch, q_heads * head_dim)]
where the time goes in v4:
time: 26.4 us; the launch traced here: 26.1 us
  Pallas kernels  22.8 us (86%)
  local copies, waits for them, and re-layouts  2.62 us (10%)
  between operations  0.65 us (2%)
    pallas_call x1, Pallas kernels, body(): pl.pallas_call(functools.partial(comm_kernel, grps, seqs, per_seq), out_s...  20 us
    pallas_call x1, Pallas kernels, body(): pl.pallas_call(functools.partial(local_kernel, per_seq, per_group, per_kv...  2.79 us
    unnamed x4, local copies, waits for them, and re-layouts  2.62 us

profile of v4, /device:TPU:15, one launch (start us, length us, event | category | flops | bytes accessed | tf_op | source)
XLA Modules:
  0.0 26.1 jit_solution(10198838999050526200)
XLA Ops:
  0.6 2.8 %local_part.1 = (bf16[32,32,256]{2,1,0:T(8,128)(2,1)}, f32[16,128]{1,0:T(8,128)}) custom-call(s32[256]{0:T(256)} %dest_ref.1, s32[8]{0:T(128)} %len_ref.1, bf16[1,32,32,256]{3,2,1,0:T(8,128)(2,1)} %lat_ref.1, bf16[8,64,128]{2,1,0:T(8,128)(2,1)} %q_ref.1, bf16[4,128,256]{2,1,0:T(8,128)(2,1)} %uk_ref.1, bf16[4,128,256]{2,1,0:T(8,128)(2,1)} %uv_ref.1), custom_call_target="tpu_custom_call" | custom-call | tf_op jit(solution)/shard_map/local_part/pallas_call | solution.py:171
  3.4 20.0 %exchange.1 = (bf16[32,32,256]{2,1,0:T(8,128)(2,1)}, f32[8,8192]{1,0:T(8,128)}) custom-call(bf16[32,32,256]{2,1,0:T(8,128)(2,1)} %get-tuple-element.6.out_ref, f32[16,128]{1,0:T(8,128)} %get-tuple-element.7.part_ref), custom_call_target="tpu_custom_call" | custom-call | tf_op jit(solution)/shard_map/exchange/pallas_call | solution.py:181
  23.4 0.0 copy-start
  23.4 1.9 %copy.10 = bf16[1,4,8,32,256]{4,3,2,1,0:T(8,128)(2,1)} copy(bf16[1,4,8,32,256]{4,3,2,1,0:T(8,128)(2,1)} %bitcast.1) | data formatting | bytes 1048576
  25.3 0.0 copy-done
  25.3 0.7 %copy.11 = f32[8,8192]{1,0:T(8,128)} copy(f32[8,8192]{1,0:T(8,128)S(1)} %copy-done) | data formatting | bytes 524288
Async XLA Ops:
  23.4 1.9 %copy-start = (f32[8,8192]{1,0:T(8,128)S(1)}, f32[8,8192]{1,0:T(8,128)}, u32[]{:S(2)}) copy-start(f32[8,8192]{1,0:T(8,128)} %get-tuple-element.13) | copy-start | bytes 786436
